TPU v7x, 256 devices: a whole 4x4x8 slice. The times are simulated.
256 devices in a mesh: layer: 4 (over y), row: 8 (over x, z_lo), col: 8 (over z_hi, core).
Axes of the slice: x: 4, y: 4, z: 8 (z_hi: 4, z_lo: 2; z = z_hi * 2 + z_lo), core: 2. Of those that a mesh axis runs over, the one named last changes fastest.
Arguments:
- ancestor: float32 [8192, 8192], P('row', 'col'), may hold values from -768 to 3840, as said below
- coupling: bfloat16 [4, 8192, 1024], P('layer', ('row', 'col')), may hold values from -10 to 10
- fronts: float32 [4, 2, 512, 512], P('layer', None, None, ('row', 'col')), may hold values from -10 to 360, as said below
- tile_pattern: int32 [4, 2, 8], P('layer'), may hold values 0 or 1
Outputs:
- schur: float32 [8192, 8192], P('row', 'col')
- panel_factor: float32 [8192, 512], P(('row', 'col'))
- pivots: float32 [512], P(('row', 'col'))
Inputs may be any that keep to these rules, and one draw needn't show every extreme that they name: `ancestor`: symmetric and positive definite; the leading [512, 512] block of schur_0 stays positive definite after all layers' terms are subtracted. `fronts`: each [512, 512] block is symmetric and positive definite, with diagonal entries from 200 to 360 and other entries within -10 to 10.
All inputs are finite; a program needn't handle non-finite values. No bound on the sum of `tile_pattern` on one device may be relied on, other than what follows from the above.
Results may differ from a plain program's by a relative error of at most 0.0008.
Values may be sent and summed in bfloat16 or wider, within the bound.
A program may use at most 128 MiB of HBM per device.

v0:
```python
import jax
import jax.numpy as jnp
from jax import lax
from jax.sharding import PartitionSpec as P

S = 8192
TILE = 1024
P_SIZE = 512
NP = 2


def spread(value, axis, source):
    kept = jnp.where(lax.axis_index(axis) == source, value, 0).astype(value.dtype)
    return lax.psum(kept, axis)


def filled_up(lines, size):
    spare = -len(lines) % size
    return jnp.pad(lines, [(0, spare)] + [(0, 0)] * (lines.ndim - 1))


def spread_2(x, axis, root):
    lines = jnp.where(lax.axis_index(axis) == root, x, jnp.zeros_like(x)).reshape(
        -1, *x.shape[1:][-1:]
    )
    padded = filled_up(lines, lax.axis_size(axis))
    own = lax.psum_scatter(padded, axis, scatter_dimension=0, tiled=True)
    return lax.all_gather(own, axis, axis=0, tiled=True)[: len(lines)].reshape(x.shape)


def column_block(sender):
    row_count = lax.axis_size("row")
    col_count = lax.axis_size("col")
    col_place = lax.axis_index("col")
    first_root = col_place * row_count // col_count
    pieces = sender(first_root + 0)
    return pieces


def solve_rows(factor, columns):
    return lax.linalg.triangular_solve(
        factor, columns, left_side=False, lower=True, transpose_a=True
    )


def local(ancestor, coupling, fronts, tile_pattern):
    row_count = lax.axis_size("row")
    col_count = lax.axis_size("col")
    row_place = lax.axis_index("row")
    col_place = lax.axis_index("col")
    local_rows = S // (row_count * col_count)
    block_rows = S // row_count
    gathered = lax.all_gather(
        fronts.astype(jnp.bfloat16), ("row", "col"), axis=3, tiled=True
    ).astype(fronts.dtype)
    factors = jnp.linalg.cholesky(gathered[0])
    first_row = (row_place * col_count + col_place) * local_rows
    positions = first_row + lax.iota(jnp.int32, local_rows)
    onehot = (positions[:, None] // TILE == lax.iota(jnp.int32, S // TILE)[None, :]).astype(
        jnp.float32
    )
    row_masks = jnp.dot(onehot, tile_pattern[0].T.astype(jnp.float32))
    solved_parts = []
    for panel in range(NP):
        columns = (
            coupling[0, :, panel * P_SIZE : (panel + 1) * P_SIZE].astype(jnp.float32)
            * row_masks[:, panel : panel + 1]
        )
        solved_parts.append(solve_rows(factors[panel], columns))
    scaled = jnp.concatenate(solved_parts, 1).astype(jnp.bfloat16)
    row_side = lax.all_gather(scaled, "col", axis=0, tiled=True)
    col_side = column_block(lambda source: spread(row_side, "row", source))
    update = -lax.dot_general(
        row_side, col_side, (((1,), (1,)), ((), ())), preferred_element_type=jnp.float32
    )
    shared = lax.psum_scatter(
        update.astype(jnp.bfloat16), "layer", scatter_dimension=0, tiled=True
    ).astype(jnp.float32)
    summed = lax.all_gather(shared.astype(jnp.bfloat16), "layer", axis=0, tiled=True).astype(
        shared.dtype
    )
    leading = ancestor[:, :P_SIZE] + summed[:, :P_SIZE]
    global_rows = row_place * block_rows + lax.iota(jnp.int32, block_rows)
    trailing = None
    working = leading
    pivot_source = working[0:P_SIZE, 0:P_SIZE]
    pivot_block = spread(pivot_source, ("row", "col"), 0)
    pivot_chol = jnp.linalg.cholesky(pivot_block)
    keep_rows = (global_rows >= 0)[:, None]
    received = spread_2(working, "col", 0)
    solved = solve_rows(pivot_chol, received)
    panel_rows = jnp.where(keep_rows, solved, jnp.zeros_like(solved))
    panel_cols = column_block(lambda source: spread(panel_rows, "row", source))
    leading = leading - jnp.dot(
        panel_rows,
        panel_cols[:P_SIZE].T,
        precision=lax.Precision.HIGHEST,
        preferred_element_type=jnp.float32,
    )
    history = (panel_rows, panel_cols)
    panel_outs = lax.dynamic_slice_in_dim(panel_rows, col_place * local_rows, local_rows, 0)
    diagonal = jnp.diagonal(pivot_chol)
    pivot_outs = diagonal * diagonal
    trailing = ancestor[:, P_SIZE:] + summed[:, P_SIZE:]
    rows_part, cols_part = history
    trailing = trailing - jnp.dot(
        rows_part,
        cols_part[P_SIZE:].T,
        precision=lax.Precision.HIGHEST,
        preferred_element_type=jnp.float32,
    )
    schur = jnp.concatenate([leading, trailing], 1)
    pivot_share = pivot_outs.shape[0] // (row_count * col_count)
    flat_place = row_place * col_count + col_place
    my_pivots = lax.dynamic_slice_in_dim(pivot_outs, flat_place * pivot_share, pivot_share, 0)
    return (schur, panel_outs, my_pivots)


def solution(mesh):
    return jax.shard_map(
        local,
        mesh=mesh,
        in_specs=(
            P("row", "col"),
            P("layer", ("row", "col"), None),
            P("layer", None, None, ("row", "col")),
            P("layer", None, None),
        ),
        out_specs=(P("row", "col"), P(("row", "col"), None), P(("row", "col"))),
        check_vma=False,
    )
```

profile of v0, /device:TPU:1, one launch (start us, length us, event | category | flops | bytes accessed | tf_op | source)
XLA Modules:
  0.0 1092.7 jit_solution(2963737448343294521)
XLA Ops:
  12.0 115.7 %all-gather.5.cloned.1.call-done = bf16[1,2,512,512]{2,3,1,0:T(8,128)(2,1)} async-done(((bf16[1,2,512,8]{2,3,1,0:T(8,128)(2,1)}), bf16[1,2,512,512]{2,3,1,0:T(8,128)(2,1)}) %all-gather.5.cloned.1.call-update) | async-done | bytes 1048592 | tf_op jit(solution)/shard_map/all_gather | solution.py:53
  134.3 23.5 %custom-call.64 = f32[2,128,128]{2,1,0:T(8,128)S(1)} custom-call(f32[2,128,128]{2,1,0:T(8,128)S(1)} %cholesky.531), custom_call_target="Cholesky" | custom-call | tf_op jit(solution)/shard_map/jit(cholesky)/cholesky | solution.py:56
  157.8 19.7 %custom-call.65 = f32[2,1,128,128]{2,3,1,0:T(8,128)S(1)} custom-call(f32[2,1,128,128]{3,2,1,0:T(8,128)S(1)} %select_bitcast_fusion.2), custom_call_target="InvertDiagBlocksLowerTriangular" | custom-call | tf_op jit(solution)/shard_map/jit(cholesky)/cholesky | solution.py:56
  180.7 23.5 %custom-call.66 = f32[2,128,128]{2,1,0:T(8,128)S(1)} custom-call(f32[2,128,128]{2,1,0:T(8,128)S(1)} %cholesky.535), custom_call_target="Cholesky" | custom-call | tf_op jit(solution)/shard_map/jit(cholesky)/cholesky | solution.py:56
  204.2 19.8 %custom-call.67 = f32[2,1,128,128]{2,3,1,0:T(8,128)S(1)} custom-call(f32[2,1,128,128]{3,2,1,0:T(8,128)S(1)} %get-tuple-element.98), custom_call_target="InvertDiagBlocksLowerTriangular" | custom-call | tf_op jit(solution)/shard_map/jit(cholesky)/cholesky | solution.py:56
  226.1 23.5 %custom-call.68 = f32[2,128,128]{2,1,0:T(8,128)S(1)} custom-call(f32[2,128,128]{2,1,0:T(8,128)S(1)} %cholesky.540), custom_call_target="Cholesky" | custom-call | tf_op jit(solution)/shard_map/jit(cholesky)/cholesky | solution.py:56
  249.5 19.7 %custom-call.69 = f32[2,1,128,128]{2,3,1,0:T(8,128)S(1)} custom-call(f32[2,1,128,128]{3,2,1,0:T(8,128)S(1)} %get-tuple-element.96), custom_call_target="InvertDiagBlocksLowerTriangular" | custom-call | tf_op jit(solution)/shard_map/jit(cholesky)/cholesky | solution.py:56
  271.0 23.7 %custom-call.70 = f32[2,128,128]{2,1,0:T(8,128)S(1)} custom-call(f32[2,128,128]{2,1,0:T(8,128)S(1)} %convolution_subtract_fusion.7), custom_call_target="Cholesky" | custom-call | tf_op jit(solution)/shard_map/jit(cholesky)/cholesky | solution.py:56
  295.8 8.5 while.6
  304.2 39.3 %custom-call.78 = f32[4,128,128]{1,2,0:T(8,128)S(1)} custom-call(f32[4,128,128]{2,1,0:T(8,128)S(1)} %get-tuple-element.26), custom_call_target="InvertDiagBlocksLowerTriangular" | custom-call | tf_op jit(solution)/shard_map/triangular_solve/custom-call.14 | solution.py:41
  343.6 8.5 while.7
  352.1 39.7 %custom-call.79 = f32[4,128,128]{1,2,0:T(8,128)S(1)} custom-call(f32[4,128,128]{2,1,0:T(8,128)S(1)} %get-tuple-element.27), custom_call_target="InvertDiagBlocksLowerTriangular" | custom-call | tf_op jit(solution)/shard_map/triangular_solve/custom-call.14 | solution.py:41
  397.4 38.6 %all-gather.7.cloned.1.call-done = bf16[1024,1024]{0,1:T(8,128)(2,1)} async-done(((bf16[128,1024]{0,1:T(8,128)(2,1)}), bf16[1024,1024]{0,1:T(8,128)(2,1)}) %all-gather.7.cloned.1.call-update) | async-done | bytes 2097168 | tf_op jit(solution)/shard_map/all_gather | solution.py:71
  437.6 108.4 %all-reduce.6.cloned.1.call-done = bf16[1024,1024]{0,1:T(8,128)(2,1)} async-done(((bf16[1024,1024]{0,1:T(8,128)(2,1)}), bf16[1024,1024]{0,1:T(8,128)(2,1)}) %all-reduce.6.cloned.1.call-update) | async-done | bytes 2097168 | tf_op jit(solution)/shard_map/psum | solution.py:14
  546.0 5.3 negate_convert_fusion
  551.4 32.3 %reduce-scatter.3.cloned.1.call-done = bf16[256,1024]{0,1:T(8,128)(2,1)} async-done(((bf16[1024,1024]{0,1:T(8,128)(2,1)}), bf16[256,1024]{0,1:T(8,128)(2,1)}) %reduce-scatter.3.cloned.1.call-update) | async-done | bytes 524304 | tf_op jit(solution)/shard_map/reduce_scatter | solution.py:76
  590.4 29.9 %all-gather.9.cloned.1.call-done = bf16[1024,1024]{0,1:T(8,128)(2,1)} async-done(((bf16[256,1024]{0,1:T(8,128)(2,1)}), bf16[1024,1024]{0,1:T(8,128)(2,1)}) %all-gather.9.cloned.1.call-update) | async-done | bytes 2097168 | tf_op jit(solution)/shard_map/all_gather | solution.py:79
  628.4 186.2 %all-reduce.8.cloned.1.call-done = f32[512,512]{0,1:T(8,128)} async-done(((f32[512,512]{0,1:T(8,128)}), f32[512,512]{0,1:T(8,128)}) %all-reduce.8.cloned.1.call-update) | async-done | bytes 1048592 | tf_op jit(solution)/shard_map/psum | solution.py:14
  816.5 11.7 %cholesky.467 = f32[128,128]{1,0:T(8,128)S(1)} custom-call(f32[128,128]{1,0:T(8,128)S(1)} %cholesky.544), custom_call_target="Cholesky" | custom-call | tf_op jit(solution)/shard_map/jit(cholesky)/cholesky | solution.py:88
  828.4 9.8 custom-call.71
  839.0 11.7 %cholesky.483 = f32[128,128]{1,0:T(8,128)S(1)} custom-call(f32[128,128]{1,0:T(8,128)S(1)} %cholesky.548), custom_call_target="Cholesky" | custom-call | tf_op jit(solution)/shard_map/jit(cholesky)/cholesky | solution.py:88
  850.8 10.0 custom-call.72
  862.0 11.7 %cholesky.504 = f32[128,128]{1,0:T(8,128)S(1)} custom-call(f32[128,128]{1,0:T(8,128)S(1)} %cholesky.553), custom_call_target="Cholesky" | custom-call | tf_op jit(solution)/shard_map/jit(cholesky)/cholesky | solution.py:88
  873.9 9.8 custom-call.73
  884.5 11.7 %cholesky.521 = f32[128,128]{1,0:T(8,128)S(1)} custom-call(f32[128,128]{1,0:T(8,128)S(1)} %convolution_subtract_fusion.12), custom_call_target="Cholesky" | custom-call | tf_op jit(solution)/shard_map/jit(cholesky)/cholesky | solution.py:88
  901.8 8.6 while.5
  910.3 39.3 %custom-call.74 = f32[4,128,128]{1,2,0:T(8,128)S(1)} custom-call(f32[4,128,128]{2,1,0:T(8,128)S(1)} %get-tuple-element.19), custom_call_target="InvertDiagBlocksLowerTriangular" | custom-call | tf_op jit(solution)/shard_map/triangular_solve | solution.py:41
  961.9 4.7 gather_fusion
  968.1 99.3 %all-reduce.10.cloned.1.call-done = f32[1024,512]{0,1:T(8,128)} async-done(((f32[1024,512]{0,1:T(8,128)}), f32[1024,512]{0,1:T(8,128)}) %all-reduce.10.cloned.1.call-update) | async-done | bytes 2097168 | tf_op jit(solution)/shard_map/psum | solution.py:14
  1067.5 5.7 convolution_subtract_fusion
  1073.2 5.0 fusion
  1080.6 5.3 copy.74
  (191 shorter events, 90.0 us)
Async XLA Ops:
  7.2 120.6 %all-gather.5.cloned.1.call-start = ((), (), s32[]{:S(2)}) async-start(), calls=%async_computation.2 | async-start | bytes 1064960 | tf_op jit(solution)/shard_map/all_gather | solution.py:53
  8.6 427.5 %all-gather.7.cloned.1.call-start = ((), (), s32[]{:S(2)}) async-start(), calls=%async_computation.3 | async-start | bytes 2359296 | tf_op jit(solution)/shard_map/all_gather | solution.py:71
  130.6 2.0 copy-start.5
  132.9 1.3 copy-start.4
  295.7 96.1 %copy-start.10 = (f32[128,512]{1,0:T(8,128)S(1)}, f32[128,512]{1,0:T(8,128)}, u32[]{:S(2)}) copy-start(f32[128,512]{1,0:T(8,128)} %get-tuple-element.93) | copy-start | bytes 786436
  295.7 98.5 %copy-start.9 = (f32[128,512]{1,0:T(8,128)S(1)}, f32[128,512]{1,0:T(8,128)}, u32[]{:S(2)}) copy-start(f32[128,512]{1,0:T(8,128)} %get-tuple-element.94) | copy-start | bytes 786436
  397.4 148.6 %all-reduce.6.cloned.1.call-start = ((), (), s32[]{:S(2)}) async-start(), calls=%async_computation.4 | async-start | bytes 4194304 | tf_op jit(solution)/shard_map/psum | solution.py:14
  437.5 108.5 %copy-start.8 = (bf16[1024,1024]{0,1:T(8,128)(2,1)S(1)}, bf16[1024,1024]{0,1:T(8,128)(2,1)}, u32[]{:S(2)}) copy-start(bf16[1024,1024]{0,1:T(8,128)(2,1)} %all-gather.7.cloned.1.call-done) | copy-start | bytes 6291460
  437.5 146.1 %reduce-scatter.3.cloned.1.call-start = ((), (), s32[]{:S(2)}) async-start(), calls=%async_computation.5 | async-start | bytes 2621440 | tf_op jit(solution)/shard_map/reduce_scatter | solution.py:76
  551.3 69.0 %all-gather.9.cloned.1.call-start = ((), (), s32[]{:S(2)}) async-start(), calls=%async_computation.6 | async-start | bytes 2621440 | tf_op jit(solution)/shard_map/all_gather | solution.py:79
  583.7 230.9 %all-reduce.8.cloned.1.call-start = ((), (), s32[]{:S(2)}) async-start(), calls=%async_computation.9 | async-start | bytes 2097152 | tf_op jit(solution)/shard_map/psum | solution.py:14
  622.4 2.7 copy-start
  625.0 1.3 copy-start.2
  627.4 233.9 %reduce-scatter.5.cloned.1.call-start = ((), (), s32[]{:S(2)}) async-start(), calls=%async_computation.7 | async-start | bytes 2359296 | tf_op jit(solution)/shard_map/reduce_scatter | solution.py:27
  628.2 321.5 %all-gather.11.cloned.1.call-start = ((), (), s32[]{:S(2)}) async-start(), calls=%async_computation.8 | async-start | bytes 2359296 | tf_op jit(solution)/shard_map/all_gather | solution.py:28
  814.6 1.7 copy-start.6
  861.4 206.1 %all-reduce.10.cloned.1.call-start = ((), (), s32[]{:S(2)}) async-start(), calls=%async_computation.10 | async-start | bytes 4194304 | tf_op jit(solution)/shard_map/psum | solution.py:14
  949.7 4.1 copy-start.7
  1067.5 5.7 copy-start.1
  1067.5 5.7 copy-start.3
Sparse Core Ops, SparseCore 0:
  10.4 117.2 all-gather.4
  397.5 38.5 all-gather.6
  439.3 106.6 all-reduce.5
  551.5 32.1 reduce-scatter.2
  585.3 34.9 all-gather.8
  627.5 187.0 all-reduce.7
  817.2 42.0 reduce-scatter.4
  861.5 40.6 all-gather.10
  959.1 108.2 all-reduce.9
where the time goes:
time: 1100 us; the launch traced here: 1090 us
  waiting for transfers between devices  611 us (56%)
  other arithmetic  371 us (34%)
  local copies, waits for them, and re-layouts  53.8 us (5%)
  matrix products  37.8 us (3%)
  between operations  17.4 us (2%)
    psum x3, waiting for transfers between devices, spread(): return lax.psum(kept, axis)  394 us
    another operation x16, other arithmetic, local(): factors = jnp.linalg.cholesky(gathered[0])  154 us
    another operation x6, other arithmetic, solve_rows(): lax.linalg.triangular_solve(factor, columns, left_side=False, lower=True,...  119 us
    all_gather x1, waiting for transfers between devices, local(): lax.all_gather(fronts.astype(jnp.bfloat16), ('row', 'col'), axis=3, tiled...  116 us
    another operation x15, other arithmetic, local(): pivot_chol = jnp.linalg.cholesky(pivot_block)  79.2 us
    all_gather x1, waiting for transfers between devices, local(): row_side = lax.all_gather(scaled, 'col', axis=0, tiled=True)  38.6 us
    reduce_scatter x1, waiting for transfers between devices, local(): lax.psum_scatter(update.astype(jnp.bfloat16), 'layer', scatter_dimension=...  32.3 us
    all_gather x1, waiting for transfers between devices, local(): lax.all_gather(shared.astype(jnp.bfloat16), 'layer', axis=0, tiled=True)  29.9 us
  transfers between devices with their start and end apart: 9, of which 7 were waited for; matrix products, arithmetic and copies ran while one was open for 14% of the time, Pallas kernels for 0%

commit v1 on v0

--- a/solution.py
+++ b/solution.py
@@ -7,6 +7,11 @@
 TILE = 1024
 P_SIZE = 512
 NP = 2
+
+
+def gather_over(block, mesh_axis, dim):
+    stack = jnp.stack([block] * lax.axis_size(mesh_axis))
+    return jnp.concatenate(lax.all_to_all(stack, mesh_axis, 0, 0), axis=dim)
 
 
 def spread(value, axis, source):
@@ -50,9 +55,7 @@
     col_place = lax.axis_index("col")
     local_rows = S // (row_count * col_count)
     block_rows = S // row_count
-    gathered = lax.all_gather(
-        fronts.astype(jnp.bfloat16), ("row", "col"), axis=3, tiled=True
-    ).astype(fronts.dtype)
+    gathered = gather_over(fronts.astype(jnp.bfloat16), ("row", "col"), 3).astype(fronts.dtype)
     factors = jnp.linalg.cholesky(gathered[0])
     first_row = (row_place * col_count + col_place) * local_rows
     positions = first_row + lax.iota(jnp.int32, local_rows)

time: 1100 us -> 1020 us (0.927)
  waiting for transfers between devices: 611 us -> 521 us
  starting transfers between devices: 0.53 us -> 13.5 us
    all_gather x1 -> x0, waiting for transfers between devices: 116 us -> none  [local(): lax.all_gather(fronts.astype(jnp.bfloat16), ('row', 'col'), axis=3, tiled...]
    all_to_all x0 -> x1, waiting for transfers between devices: none -> 26.2 us  [gather_over(): return jnp.concatenate(lax.all_to_all(stack, mesh_axis, 0, 0), axis=dim)]
    all_to_all x0 -> x1, starting transfers between devices: none -> 13 us  [gather_over(): return jnp.concatenate(lax.all_to_all(stack, mesh_axis, 0, 0), axis=dim)]
  transfers between devices with their start and end apart: 9 -> 9, of which waited for: 7 -> 7; matrix products, arithmetic and copies ran while one was open for 14% -> 15% of each run, Pallas kernels for 0% -> 0%
where the time goes in v1:
time: 1020 us; the launch traced here: 1010 us
  waiting for transfers between devices  521 us (51%)
  other arithmetic  368 us (36%)
  local copies, waits for them, and re-layouts  54.1 us (5%)
  matrix products  37.1 us (4%)
  between operations  17.7 us (2%)
  starting transfers between devices  13.5 us (1%)
    psum x3, waiting for transfers between devices, spread(): return lax.psum(kept, axis)  394 us
    another operation x16, other arithmetic, local(): factors = jnp.linalg.cholesky(gathered[0])  154 us
    another operation x6, other arithmetic, solve_rows(): lax.linalg.triangular_solve(factor, columns, left_side=False, lower=True,...  119 us
    another operation x15, other arithmetic, local(): pivot_chol = jnp.linalg.cholesky(pivot_block)  79.2 us
    all_gather x1, waiting for transfers between devices, local(): row_side = lax.all_gather(scaled, 'col', axis=0, tiled=True)  38.1 us
    reduce_scatter x1, waiting for transfers between devices, local(): lax.psum_scatter(update.astype(jnp.bfloat16), 'layer', scatter_dimension=...  32.3 us
    all_gather x1, waiting for transfers between devices, local(): lax.all_gather(shared.astype(jnp.bfloat16), 'layer', axis=0, tiled=True)  29.9 us
    all_to_all x1, waiting for transfers between devices, gather_over(): return jnp.concatenate(lax.all_to_all(stack, mesh_axis, 0, 0), axis=dim)  26.2 us
  transfers between devices with their start and end apart: 9, of which 7 were waited for; matrix products, arithmetic and copies ran while one was open for 15% of the time, Pallas kernels for 0%

profile of v1, /device:TPU:1, one launch (start us, length us, event | category | flops | bytes accessed | tf_op | source)
XLA Modules:
  0.0 1012.7 jit_solution(285605418660654034)
XLA Ops:
  9.1 13.0 %all-to-all-start = ((bf16[64,1,2,512,8]{3,4,2,1,0:T(8,128)(2,1)}), bf16[64,1,2,512,8]{3,4,2,1,0:T(8,128)(2,1)S(1)}, u32[]{:S(2)}, u32[]{:S(2)}) async-start(bf16[64,1,2,512,8]{3,4,2,1,0:T(8,128)(2,1)} %stack.2), calls=%async_computation | async-start | bytes 2097152 | tf_op jit(solution)/shard_map/all_to_all | solution.py:14
  23.8 26.2 %all-to-all-done = bf16[64,1,2,512,8]{3,4,2,1,0:T(8,128)(2,1)S(1)} async-done(((bf16[64,1,2,512,8]{3,4,2,1,0:T(8,128)(2,1)}), bf16[64,1,2,512,8]{3,4,2,1,0:T(8,128)(2,1)S(1)}, u32[]{:S(2)}, u32[]{:S(2)}) %all-to-all-start) | async-done | bytes 1048608 | tf_op jit(solution)/shard_map/all_to_all | solution.py:14
  55.2 23.5 %custom-call.64 = f32[2,128,128]{2,1,0:T(8,128)S(1)} custom-call(f32[2,128,128]{2,1,0:T(8,128)S(1)} %cholesky.531), custom_call_target="Cholesky" | custom-call | tf_op jit(solution)/shard_map/jit(cholesky)/cholesky | solution.py:59
  78.7 19.7 %custom-call.65 = f32[2,1,128,128]{2,3,1,0:T(8,128)S(1)} custom-call(f32[2,1,128,128]{3,2,1,0:T(8,128)S(1)} %select_bitcast_fusion.2), custom_call_target="InvertDiagBlocksLowerTriangular" | custom-call | tf_op jit(solution)/shard_map/jit(cholesky)/cholesky | solution.py:59
  101.7 23.5 %custom-call.66 = f32[2,128,128]{2,1,0:T(8,128)S(1)} custom-call(f32[2,128,128]{2,1,0:T(8,128)S(1)} %cholesky.535), custom_call_target="Cholesky" | custom-call | tf_op jit(solution)/shard_map/jit(cholesky)/cholesky | solution.py:59
  125.2 19.8 %custom-call.67 = f32[2,1,128,128]{2,3,1,0:T(8,128)S(1)} custom-call(f32[2,1,128,128]{3,2,1,0:T(8,128)S(1)} %get-tuple-element.105), custom_call_target="InvertDiagBlocksLowerTriangular" | custom-call | tf_op jit(solution)/shard_map/jit(cholesky)/cholesky | solution.py:59
  147.0 23.5 %custom-call.68 = f32[2,128,128]{2,1,0:T(8,128)S(1)} custom-call(f32[2,128,128]{2,1,0:T(8,128)S(1)} %cholesky.540), custom_call_target="Cholesky" | custom-call | tf_op jit(solution)/shard_map/jit(cholesky)/cholesky | solution.py:59
  170.5 19.7 %custom-call.69 = f32[2,1,128,128]{2,3,1,0:T(8,128)S(1)} custom-call(f32[2,1,128,128]{3,2,1,0:T(8,128)S(1)} %get-tuple-element.103), custom_call_target="InvertDiagBlocksLowerTriangular" | custom-call | tf_op jit(solution)/shard_map/jit(cholesky)/cholesky | solution.py:59
  192.0 23.7 %custom-call.70 = f32[2,128,128]{2,1,0:T(8,128)S(1)} custom-call(f32[2,128,128]{2,1,0:T(8,128)S(1)} %convolution_subtract_fusion.7), custom_call_target="Cholesky" | custom-call | tf_op jit(solution)/shard_map/jit(cholesky)/cholesky | solution.py:59
  216.7 8.0 while.6
  224.7 39.3 %custom-call.78 = f32[4,128,128]{1,2,0:T(8,128)S(1)} custom-call(f32[4,128,128]{2,1,0:T(8,128)S(1)} %get-tuple-element.26), custom_call_target="InvertDiagBlocksLowerTriangular" | custom-call | tf_op jit(solution)/shard_map/triangular_solve/custom-call.14 | solution.py:46
  264.1 8.1 while.7
  272.2 39.7 %custom-call.79 = f32[4,128,128]{1,2,0:T(8,128)S(1)} custom-call(f32[4,128,128]{2,1,0:T(8,128)S(1)} %get-tuple-element.27), custom_call_target="InvertDiagBlocksLowerTriangular" | custom-call | tf_op jit(solution)/shard_map/triangular_solve/custom-call.14 | solution.py:46
  317.6 38.1 %all-gather.4.cloned.1.call-done = bf16[1024,1024]{0,1:T(8,128)(2,1)} async-done(((bf16[128,1024]{0,1:T(8,128)(2,1)}), bf16[1024,1024]{0,1:T(8,128)(2,1)}) %all-gather.4.cloned.1.call-update) | async-done | bytes 2097168 | tf_op jit(solution)/shard_map/all_gather | solution.py:74
  357.3 108.4 %all-reduce.6.cloned.1.call-done = bf16[1024,1024]{0,1:T(8,128)(2,1)} async-done(((bf16[1024,1024]{0,1:T(8,128)(2,1)}), bf16[1024,1024]{0,1:T(8,128)(2,1)}) %all-reduce.6.cloned.1.call-update) | async-done | bytes 2097168 | tf_op jit(solution)/shard_map/psum | solution.py:19
  465.7 5.3 negate_convert_fusion
  471.1 32.3 %reduce-scatter.3.cloned.1.call-done = bf16[256,1024]{0,1:T(8,128)(2,1)} async-done(((bf16[1024,1024]{0,1:T(8,128)(2,1)}), bf16[256,1024]{0,1:T(8,128)(2,1)}) %reduce-scatter.3.cloned.1.call-update) | async-done | bytes 524304 | tf_op jit(solution)/shard_map/reduce_scatter | solution.py:79
  510.0 29.9 %all-gather.6.cloned.1.call-done = bf16[1024,1024]{0,1:T(8,128)(2,1)} async-done(((bf16[256,1024]{0,1:T(8,128)(2,1)}), bf16[1024,1024]{0,1:T(8,128)(2,1)}) %all-gather.6.cloned.1.call-update) | async-done | bytes 2097168 | tf_op jit(solution)/shard_map/all_gather | solution.py:82
  547.9 186.4 %all-reduce.8.cloned.1.call-done = f32[512,512]{0,1:T(8,128)} async-done(((f32[512,512]{0,1:T(8,128)}), f32[512,512]{0,1:T(8,128)}) %all-reduce.8.cloned.1.call-update) | async-done | bytes 1048592 | tf_op jit(solution)/shard_map/psum | solution.py:19
  736.2 11.7 %cholesky.467 = f32[128,128]{1,0:T(8,128)S(1)} custom-call(f32[128,128]{1,0:T(8,128)S(1)} %cholesky.544), custom_call_target="Cholesky" | custom-call | tf_op jit(solution)/shard_map/jit(cholesky)/cholesky | solution.py:91
  748.0 9.8 custom-call.71
  758.7 11.7 %cholesky.483 = f32[128,128]{1,0:T(8,128)S(1)} custom-call(f32[128,128]{1,0:T(8,128)S(1)} %cholesky.548), custom_call_target="Cholesky" | custom-call | tf_op jit(solution)/shard_map/jit(cholesky)/cholesky | solution.py:91
  770.5 10.0 custom-call.72
  781.7 11.7 %cholesky.504 = f32[128,128]{1,0:T(8,128)S(1)} custom-call(f32[128,128]{1,0:T(8,128)S(1)} %cholesky.553), custom_call_target="Cholesky" | custom-call | tf_op jit(solution)/shard_map/jit(cholesky)/cholesky | solution.py:91
  793.6 9.8 custom-call.73
  804.2 11.7 %cholesky.521 = f32[128,128]{1,0:T(8,128)S(1)} custom-call(f32[128,128]{1,0:T(8,128)S(1)} %convolution_subtract_fusion.12), custom_call_target="Cholesky" | custom-call | tf_op jit(solution)/shard_map/jit(cholesky)/cholesky | solution.py:91
  821.4 8.6 while.5
  830.0 39.3 %custom-call.74 = f32[4,128,128]{1,2,0:T(8,128)S(1)} custom-call(f32[4,128,128]{2,1,0:T(8,128)S(1)} %get-tuple-element.19), custom_call_target="InvertDiagBlocksLowerTriangular" | custom-call | tf_op jit(solution)/shard_map/triangular_solve | solution.py:46
  887.8 99.3 %all-reduce.10.cloned.1.call-done = f32[1024,512]{0,1:T(8,128)} async-done(((f32[1024,512]{0,1:T(8,128)}), f32[1024,512]{0,1:T(8,128)}) %all-reduce.10.cloned.1.call-update) | async-done | bytes 2097168 | tf_op jit(solution)/shard_map/psum | solution.py:19
  987.1 5.7 convolution_subtract_fusion
  992.8 5.0 fusion
  1000.3 5.3 copy.101
  (193 shorter events, 91.2 us)
Async XLA Ops:
  7.2 15.5 %copy-start.11 = (s32[1,2,8]{2,1,0:T(2,128)S(1)}, s32[1,2,8]{2,1,0:T(2,128)}, u32[]{:S(2)}) copy-start(s32[1,2,8]{2,1,0:T(2,128)} %param.9) | copy-start | bytes 196
  7.2 15.7 %copy-start.10 = (bf16[1,128,1024]{2,1,0:T(8,128)(2,1)S(1)}, bf16[1,128,1024]{2,1,0:T(8,128)(2,1)}, u32[]{:S(2)}) copy-start(bf16[1,128,1024]{2,1,0:T(8,128)(2,1)} %param.7) | copy-start | bytes 786436
  9.1 40.9 %all-to-all-start = ((bf16[64,1,2,512,8]{3,4,2,1,0:T(8,128)(2,1)}), bf16[64,1,2,512,8]{3,4,2,1,0:T(8,128)(2,1)S(1)}, u32[]{:S(2)}, u32[]{:S(2)}) async-start(bf16[64,1,2,512,8]{3,4,2,1,0:T(8,128)(2,1)} %stack.2), calls=%async_computation | async-start | bytes 2097152 | tf_op jit(solution)/shard_map/all_to_all | solution.py:14
  22.1 333.6 %all-gather.4.cloned.1.call-start = ((), (), s32[]{:S(2)}) async-start(), calls=%async_computation.3 | async-start | bytes 2359296 | tf_op jit(solution)/shard_map/all_gather | solution.py:74
  53.9 1.3 copy-start.4
  216.6 95.3 %copy-start.9 = (f32[128,512]{1,0:T(8,128)S(1)}, f32[128,512]{1,0:T(8,128)}, u32[]{:S(2)}) copy-start(f32[128,512]{1,0:T(8,128)} %get-tuple-element.100) | copy-start | bytes 786436
  216.7 97.7 %copy-start.8 = (f32[128,512]{1,0:T(8,128)S(1)}, f32[128,512]{1,0:T(8,128)}, u32[]{:S(2)}) copy-start(f32[128,512]{1,0:T(8,128)} %get-tuple-element.101) | copy-start | bytes 786436
  317.5 148.2 %all-reduce.6.cloned.1.call-start = ((), (), s32[]{:S(2)}) async-start(), calls=%async_computation.4 | async-start | bytes 4194304 | tf_op jit(solution)/shard_map/psum | solution.py:19
  357.2 108.5 %copy-start.7 = (bf16[1024,1024]{0,1:T(8,128)(2,1)S(1)}, bf16[1024,1024]{0,1:T(8,128)(2,1)}, u32[]{:S(2)}) copy-start(bf16[1024,1024]{0,1:T(8,128)(2,1)} %all-gather.4.cloned.1.call-done) | copy-start | bytes 6291460
  357.2 146.1 %reduce-scatter.3.cloned.1.call-start = ((), (), s32[]{:S(2)}) async-start(), calls=%async_computation.5 | async-start | bytes 2621440 | tf_op jit(solution)/shard_map/reduce_scatter | solution.py:79
  471.0 69.0 %all-gather.6.cloned.1.call-start = ((), (), s32[]{:S(2)}) async-start(), calls=%async_computation.6 | async-start | bytes 2621440 | tf_op jit(solution)/shard_map/all_gather | solution.py:82
  503.3 230.9 %all-reduce.8.cloned.1.call-start = ((), (), s32[]{:S(2)}) async-start(), calls=%async_computation.9 | async-start | bytes 2097152 | tf_op jit(solution)/shard_map/psum | solution.py:19
  542.0 2.7 copy-start
  544.7 1.3 copy-start.2
  547.1 233.9 %reduce-scatter.5.cloned.1.call-start = ((), (), s32[]{:S(2)}) async-start(), calls=%async_computation.7 | async-start | bytes 2359296 | tf_op jit(solution)/shard_map/reduce_scatter | solution.py:32
  547.7 321.7 %all-gather.8.cloned.1.call-start = ((), (), s32[]{:S(2)}) async-start(), calls=%async_computation.8 | async-start | bytes 2359296 | tf_op jit(solution)/shard_map/all_gather | solution.py:33
  734.3 1.7 copy-start.5
  781.0 206.1 %all-reduce.10.cloned.1.call-start = ((), (), s32[]{:S(2)}) async-start(), calls=%async_computation.10 | async-start | bytes 4194304 | tf_op jit(solution)/shard_map/psum | solution.py:19
  869.3 4.1 copy-start.6
  987.1 5.7 copy-start.1
  987.1 5.7 copy-start.3
Sparse Core Ops, SparseCore 0:
  317.6 38.0 all-gather.3
  358.9 106.6 all-reduce.5
  471.1 32.1 reduce-scatter.2
  505.0 34.9 all-gather.5
  547.2 187.0 all-reduce.7
  736.7 41.5 reduce-scatter.4
  781.2 41.0 all-gather.7
  878.8 108.2 all-reduce.9
